TPU v7x, 128 devices: a whole 4x4x4 slice. The times are simulated.
128 devices in a mesh: scen: 8 (over x_hi, y), slab: 16 (over z, x_lo, core).
Axes of the slice: x: 4 (x_hi: 2, x_lo: 2; x = x_hi * 2 + x_lo), y: 4, z: 4, core: 2. Of those that a mesh axis runs over, the one named last changes fastest.
Arguments:
- start: float32 [8, 128, 256, 256], P('scen', 'slab'), may hold values from 0 to 2
- flow_east: float32 [8, 128, 256, 256], P('scen', 'slab'), may hold values from 0.3 to 1.2
- flow_north: float32 [8, 128, 256, 256], P('scen', 'slab'), may hold values from 0.3 to 1.2
- wells: int32 [128, 256, 256], P('slab'), may hold values 0 or 1
- monitors: int32 [128, 256, 256], P('slab'), may hold values 0 or 1
- control: float32 [8, 32, 4096], P('scen', 'slab'), may hold values from -3 to 3
- multiplier: float32 [8, 32, 4096], P('scen', 'slab'), may hold values from -3 to 3
- threshold: float32 [1], replicated, may hold values from 0.8 to 1.3
Outputs:
- final_fields: float32 [8, 128, 256, 256], P('scen', 'slab')
- consensus_next: float32 [32, 4096], P('slab')
- multiplier_next: float32 [8, 32, 4096], P('scen', 'slab')
- cvar: float32 [1], replicated
All inputs are finite; a program needn't handle non-finite values. No bound on the sum of `wells` or of `monitors` on one device may be relied on, other than what follows from the above.
Results may differ from a plain program's by a relative error of at most 0.00002.
Values sent between devices are 32-bit elements; how exact they have to be, the bound alone decides.
No kernel may reach another device: no remote copies, remote signals or barrier semaphores. Data moves between devices by JAX's collectives and lax.ppermute only.
A program may use at most 192 MiB of HBM per device.

v0:
```python
import jax
import jax.numpy as jnp
from jax import lax
from jax.sharding import PartitionSpec as P

STEPS = 4
EPS_LIMIT = 0.01
TIME_STEP = 0.25
DIFF_FLAT = 0.1
DIFF_VERTICAL = 0.25
BETA_LEVEL = 0.75
SOFT_WIDTH = 0.25


def with_halo(cells, sides, width):
    for axis, dim in sides:
        count = lax.axis_size(axis)
        ends = count - 1
        head = lax.slice_in_dim(cells, 0, width, axis=dim)
        tail = lax.slice_in_dim(cells, cells.shape[dim] - width, cells.shape[dim], axis=dim)
        cells = jnp.concatenate(
            [
                lax.ppermute(tail, axis, [(i, (i + 1) % count) for i in range(ends)]),
                cells,
                lax.ppermute(head, axis, [((i + 1) % count, i) for i in range(ends)]),
            ],
            axis=dim,
        )
    return cells


def pad_axis(field, which_axis, low_pad, high_pad):
    widths = [(0, 0)] * field.ndim
    widths[which_axis] = (low_pad, high_pad)
    return jnp.pad(field, widths)


def second_difference(padded, field, which_axis):
    length = field.shape[which_axis]
    upper_cells = lax.slice_in_dim(padded, 2, length + 2, axis=which_axis)
    lower_cells = lax.slice_in_dim(padded, 0, length, axis=which_axis)
    return upper_cells - 2.0 * field + lower_cells


def divergence(field, velocity, which_axis):
    length = field.shape[which_axis]
    padded = pad_axis(field, which_axis, 1, 1)
    lower_cells = lax.slice_in_dim(padded, 0, length, axis=which_axis)
    upper_cells = lax.slice_in_dim(padded, 2, length + 2, axis=which_axis)
    backward = field - lower_cells
    forward = upper_cells - field
    product = backward * forward
    weight = (product + jnp.sqrt(product * product + EPS_LIMIT * EPS_LIMIT)) / (
        backward * backward + forward * forward + EPS_LIMIT
    )
    face_value = field + 0.5 * weight * (backward / 3.0 + 2.0 * forward / 3.0)
    fluxes = velocity * face_value
    previous = lax.slice_in_dim(pad_axis(fluxes, which_axis, 1, 0), 0, length, axis=which_axis)
    return fluxes - previous


def horizontal(field, flow_east, flow_north, rate):
    advect = divergence(field, flow_east, 1) + divergence(field, flow_north, 2)
    spread = second_difference(pad_axis(field, 1, 1, 1), field, 1) + second_difference(
        pad_axis(field, 2, 1, 1), field, 2
    )
    return -advect + DIFF_FLAT * spread - rate * field


def prolong(coarse, row_count, column_count):
    plane_count = coarse.shape[0]
    cube = coarse.reshape(plane_count, 1, row_count // 4, 1, column_count // 4, 1)
    cube = jnp.broadcast_to(cube, (plane_count, 4, row_count // 4, 4, column_count // 4, 4))
    return cube.reshape(plane_count * 4, row_count, column_count)


def restrict(fine):
    plane_count, row_count, column_count = fine.shape
    blocks = fine.reshape(plane_count // 4, 4, row_count // 4, 4, column_count // 4, 4).sum(
        axis=(1, 3, 5)
    )
    return blocks.reshape(plane_count // 4, row_count // 4 * (column_count // 4))


def on_device(start, flow_east, flow_north, wells, monitors, control, multiplier, threshold):
    scen_count = lax.axis_size("scen")
    slab_count = lax.axis_size("slab")
    consensus = lax.psum(jnp.sum(control + multiplier, axis=0), "scen") / scen_count
    field = start[0]
    east = flow_east[0]
    north = flow_north[0]
    plane_count, row_count, column_count = field.shape
    wells_float = wells.astype(jnp.float32)
    monitor_float = monitors.astype(jnp.float32)
    rate = wells_float * prolong(consensus, row_count, column_count)
    states = []
    for step_index in range(STEPS):
        states.append(field)
        padded = with_halo(field, (("slab", 0),), 1)
        vertical = second_difference(padded, field, 0)
        field = field + TIME_STEP * (
            horizontal(field, east, north, rate) + DIFF_VERTICAL * vertical
        )
    mass, count = lax.psum((jnp.sum(monitor_float * field * field), jnp.sum(monitor_float)), "slab")
    count = jnp.maximum(count, 1.0)
    loss = mass / count
    scaled = (loss - threshold[0]) / SOFT_WIDTH
    weight = jax.nn.sigmoid(scaled) / ((1.0 - BETA_LEVEL) * scen_count)
    soft_term = SOFT_WIDTH * jax.nn.softplus(scaled) / ((1.0 - BETA_LEVEL) * scen_count)
    risk = lax.psum(soft_term, "scen")
    adjoint = weight * 2.0 * monitor_float * field / count
    rate_grad = jnp.zeros_like(field)
    for step_index in reversed(range(STEPS)):
        state = states[step_index]
        padded = with_halo(adjoint, (("slab", 0),), 1)
        unused, pullback = jax.vjp(lambda values: horizontal(values, east, north, rate), state)
        (pulled,) = pullback(adjoint)
        rate_grad = rate_grad - TIME_STEP * state * adjoint
        vertical = second_difference(padded, adjoint, 0)
        adjoint = adjoint + TIME_STEP * (pulled + DIFF_VERTICAL * vertical)
    coarse_cells = plane_count * slab_count * row_count * column_count / 64.0
    gradient = coarse_cells * restrict(wells_float * rate_grad)
    total = lax.psum(gradient, "scen")
    consensus_next = consensus - total
    multiplier_next = multiplier + control - consensus_next[None]
    cvar = threshold + risk
    return (field[None], consensus_next, multiplier_next, cvar)


def solution(mesh):
    placed = (
        P("scen", "slab", None, None),
        P("scen", "slab", None, None),
        P("scen", "slab", None, None),
        P("slab", None, None),
        P("slab", None, None),
        P("scen", "slab", None),
        P("scen", "slab", None),
        P(),
    )
    return jax.shard_map(
        on_device,
        mesh=mesh,
        in_specs=placed,
        out_specs=(P("scen", "slab", None, None), P("slab", None), P("scen", "slab", None), P()),
        check_vma=False,
    )
```

profile of v0, /device:TPU:2, one launch (start us, length us, event | category | flops | bytes accessed | tf_op | source)
XLA Modules:
  0.0 485.9 jit_solution(5351484315725654341)
XLA Ops:
  3.6 2.4 collective-permute-start.1
  6.9 41.1 %psum.35 = f32[2,4096]{1,0:T(2,128)S(1)} all-reduce(f32[2,4096]{1,0:T(2,128)S(1)} %bitcast.40), channel_id=1, replica_groups=mesh['scen'=8,'slab'=16] {'scen'}, use_global_device_ids=true, to_apply=%region_0.0 | all-reduce | flops 8192 | bytes 65536 | tf_op jit(solution)/shard_map/psum | solution.py:88
  48.0 11.3 %bitcast_multiply_fusion.3 = (f32[8,256,256]{2,1,0:T(8,128)}, f32[8,256,256]{2,1,0:T(8,128)}) fusion(f32[1,8,256,256]{3,2,1,0:T(8,128)} %param.10, f32[8,256,256]{2,1,0:T(8,128)} %bitcast.37, f32[1,8,256,256]{3,2,1,0:T(8,128)} %param.9), kind=kLoop, calls=%fused_computation.197 | loop fusion | flops 18874368 | bytes 10485760 | tf_op jit(solution)/shard_map/mul | solution.py:57
  59.4 21.5 %broadcast_in_dim.17 = f32[2,4,64,4,64,4]{5,4,3,2,1,0:T(8,128)} broadcast(f32[2,64,64]{2,1,0:T(8,128)S(1)} %broadcast_in_dim.16), dimensions={0,2,4} | broadcast | bytes 2129920 | tf_op jit(solution)/shard_map/broadcast_in_dim | solution.py:73
  80.9 56.1 %reshape.22 = f32[8,256,256]{2,1,0:T(8,128)} reshape(f32[2,4,64,4,64,4]{5,4,3,2,1,0:T(8,128)} %broadcast_in_dim.17) | data formatting | bytes 4194304 | tf_op jit(solution)/shard_map/reshape | solution.py:74
  137.7 12.0 %fusion.7 = (f32[8,256,256]{2,1,0:T(8,128)S(1)}, f32[8,256,256]{2,1,0:T(8,128)S(1)}) fusion(f32[8,256,256]{2,1,0:T(8,128)} %bitcast.38, f32[8,256,256]{2,1,0:T(8,128)} %get-tuple-element.78, f32[8,256,256]{2,1,0:T(8,128)} %get-tuple-element.77, f32[1,256,256]{2,1,0:T(8,128)S(1)} %collective-permute-done.1, f32[1,256,256]{2,1,0:T(8,128)S(1)} %collective-permute-done, ...), kind=kLoop, calls=%fused_computation.48 | loop fusion | flops 12582912 | bytes 15204352 | tf_op jit(solution)/shard_map/add | solution.py:101
  154.1 4.1 bitcast_multiply_fusion.2
  159.4 3.2 fusion.15
  164.7 3.4 collective-permute-start.5
  168.0 4.1 bitcast_multiply_fusion.1
  172.4 3.0 fusion.23
  177.9 4.1 collective-permute-start.7
  182.0 4.1 bitcast_multiply_fusion.4
  186.2 5.0 %fusion.42 = (f32[]{:T(128)}, f32[]{:T(128)}, f32[8,256,256]{2,1,0:T(8,128)}) fusion(s32[8,256,256]{2,1,0:T(8,128)S(1)} %copy-done.21, f32[8,256,256]{2,1,0:T(8,128)S(1)} %fusion.23, f32[1,256,256]{2,1,0:T(8,128)S(1)} %collective-permute-done.7, f32[1,256,256]{2,1,0:T(8,128)S(1)} %collective-permute-done.6, f32[8,256,256]{2,1,0:T(8,128)S(1)} %get-tuple-element.44, ...), kind=kLoop, calls=%fused_computation.83 | loop fusion | flops 14155774 | bytes 13107208 | tf_op jit(solution)/shard_map/reduce_sum | solution.py:104
  191.2 27.7 %all-reduce.46 = (f32[]{:T(128)}, f32[]{:T(128)}) all-reduce(f32[]{:T(128)} %get-tuple-element.5, f32[]{:T(128)} %get-tuple-element.4), channel_id=1, replica_groups=mesh['scen'=8,'slab'=16] {'slab'}, use_global_device_ids=true, to_apply=%region_4.5 | all-reduce | flops 2 | bytes 16 | tf_op jit(solution)/shard_map/psum | solution.py:104
  220.2 4.4 broadcast_multiply_fusion.2
  224.6 8.3 %fusion.45 = (f32[8,256,256]{2,1,0:T(8,128)}, f32[8,256,256]{2,1,0:T(8,128)S(1)}, f32[8,256,256]{2,1,0:T(8,128)}, f32[8,256,256]{2,1,0:T(8,128)S(1)}) fusion(f32[8,256,256]{2,1,0:T(8,128)S(1)} %copy-done.10, f32[8,256,256]{2,1,0:T(8,128)S(1)} %get-tuple-element.33, f32[1,8,256,256]{3,2,1,0:T(8,128)S(1)} %copy-done, f32[1,8,256,256]{3,2,1,0:T(8,128)S(1)} %copy-done.2), kind=kLoop, calls=%fused_computation.86 | loop fusion | flops 39321600 | bytes 16777216 | tf_op jit(solution)/shard_map/transpose(jvp())/add_any | solution.py:52
  232.9 5.3 %collective-permute-start.8 = (f32[1,256,256]{2,1,0:T(8,128)S(1)}, f32[1,256,256]{2,1,0:T(8,128)S(1)}, u32[]{:S(2)}, u32[]{:S(2)}) collective-permute-start(f32[1,256,256]{2,1,0:T(8,128)S(1)} %get-tuple-element.61), channel_id=1, source_target_pairs={{1,0},{2,1},{3,2},{4,3},{5,4},{6,5},{7,6},{8,7},{9,8},{10,9},{11,1... | collective-permute-start | bytes 786440 | tf_op jit(solution)/shard_map/ppermute | solution.py:25
  238.2 2.4 collective-permute-start.9
  240.7 8.5 %fusion.190 = (f32[8,256,256]{2,1,0:T(8,128)}, f32[8,256,256]{2,1,0:T(8,128)}, f32[8,256,256]{2,1,0:T(8,128)}, f32[8,256,256]{2,1,0:T(8,128)}) fusion(f32[8,256,256]{2,1,0:T(8,128)S(1)} %get-tuple-element.35, f32[8,256,256]{2,1,0:T(8,128)S(1)} %copy-done.10, f32[8,256,256]{2,1,0:T(8,128)S(1)} %get-tuple-element.50), kind=kLoop, calls=%fused_computation.312 | loop fusion | flops 37748736 | bytes 14680064 | tf_op jit(solution)/shard_map/transpose(jvp())/neg | solution.py:50
  249.4 16.8 %broadcast_multiply_fusion.1 = (f32[8,256,256]{2,1,0:T(8,128)}, f32[8,256,256]{2,1,0:T(8,128)S(1)}) fusion(f32[8,256,256]{2,1,0:T(8,128)} %copy-done.13, f32[1,256,256]{2,1,0:T(8,128)S(1)} %collective-permute-done.9, f32[1,256,256]{2,1,0:T(8,128)S(1)} %collective-permute-done.8, f32[8,256,256]{2,1,0:T(8,128)} %get-tuple-element.59, ...), kind=kLoop, calls=%fused_computation.294 | loop fusion | flops 16777216 | bytes 27787264 | tf_op jit(solution)/shard_map/transpose(jvp())/mul | solution.py:67
  266.2 8.3 %fusion.51 = (f32[8,256,256]{2,1,0:T(8,128)}, f32[8,256,256]{2,1,0:T(8,128)S(1)}, f32[8,256,256]{2,1,0:T(8,128)}, f32[8,256,256]{2,1,0:T(8,128)S(1)}) fusion(f32[8,256,256]{2,1,0:T(8,128)S(1)} %copy-done.8, f32[8,256,256]{2,1,0:T(8,128)S(1)} %get-tuple-element.23, f32[1,8,256,256]{3,2,1,0:T(8,128)S(1)} %copy-done, f32[1,8,256,256]{3,2,1,0:T(8,128)S(1)} %copy-done.3), kind=kLoop, calls=%fused_computation.92 | loop fusion | flops 39321600 | bytes 16777216 | tf_op jit(solution)/shard_map/transpose(jvp())/add_any | solution.py:52
  274.5 3.6 collective-permute-start.10
  280.3 8.4 %fusion.184 = (f32[8,256,256]{2,1,0:T(8,128)}, f32[8,256,256]{2,1,0:T(8,128)}, f32[8,256,256]{2,1,0:T(8,128)}, f32[8,256,256]{2,1,0:T(8,128)}) fusion(f32[8,256,256]{2,1,0:T(8,128)S(1)} %get-tuple-element.25, f32[8,256,256]{2,1,0:T(8,128)S(1)} %copy-done.8, f32[8,256,256]{2,1,0:T(8,128)S(1)} %get-tuple-element.48), kind=kLoop, calls=%fused_computation.310 | loop fusion | flops 37748736 | bytes 14680064 | tf_op jit(solution)/shard_map/transpose(jvp())/neg | solution.py:50
  288.8 16.4 %broadcast_multiply_fusion = (f32[8,256,256]{2,1,0:T(8,128)}, f32[8,256,256]{2,1,0:T(8,128)}) fusion(f32[8,256,256]{2,1,0:T(8,128)} %copy-done.14, f32[1,256,256]{2,1,0:T(8,128)S(1)} %collective-permute-done.11, f32[1,256,256]{2,1,0:T(8,128)S(1)} %collective-permute-done.10, f32[8,256,256]{2,1,0:T(8,128)} %get-tuple-element.55, ...), kind=kLoop, calls=%fused_computation.293 | loop fusion | flops 16777216 | bytes 27787264 | tf_op jit(solution)/shard_map/transpose(jvp())/mul | solution.py:67
  305.2 10.2 %fusion.57 = (f32[8,256,256]{2,1,0:T(8,128)}, f32[8,256,256]{2,1,0:T(8,128)S(1)}, f32[8,256,256]{2,1,0:T(8,128)}, f32[8,256,256]{2,1,0:T(8,128)S(1)}) fusion(f32[8,256,256]{2,1,0:T(8,128)S(1)} %copy-done.12, f32[8,256,256]{2,1,0:T(8,128)} %get-tuple-element.13, f32[1,8,256,256]{3,2,1,0:T(8,128)S(1)} %copy-done, f32[1,8,256,256]{3,2,1,0:T(8,128)S(1)} %copy-done.3), kind=kLoop, calls=%fused_computation.98 | loop fusion | flops 39321600 | bytes 16777216 | tf_op jit(solution)/shard_map/transpose(jvp())/add_any | solution.py:52
  316.8 3.6 collective-permute-start.12
  322.6 8.5 %fusion.177 = (f32[8,256,256]{2,1,0:T(8,128)}, f32[8,256,256]{2,1,0:T(8,128)}, f32[8,256,256]{2,1,0:T(8,128)}, f32[8,256,256]{2,1,0:T(8,128)}) fusion(f32[8,256,256]{2,1,0:T(8,128)S(1)} %get-tuple-element.15, f32[8,256,256]{2,1,0:T(8,128)S(1)} %copy-done.12, f32[8,256,256]{2,1,0:T(8,128)S(1)} %get-tuple-element.46), kind=kLoop, calls=%fused_computation.308 | loop fusion | flops 37748736 | bytes 14680064 | tf_op jit(solution)/shard_map/transpose(jvp())/neg | solution.py:50
  331.1 21.2 %fusion.68 = f32[8,256,256]{2,1,0:T(8,128)} fusion(f32[8,256,256]{2,1,0:T(8,128)} %get-tuple-element.13, f32[1,256,256]{2,1,0:T(8,128)S(1)} %collective-permute-done.13, f32[1,256,256]{2,1,0:T(8,128)S(1)} %collective-permute-done.12, f32[8,256,256]{2,1,0:T(8,128)} %get-tuple-element.51, f32[8,256,256]{2,1,0:T(8,128)} %get-tuple-element.45, ...), kind=kLoop, calls=%fused_computation.110 | loop fusion | flops 23592960 | bytes 40370176 | tf_op jit(solution)/shard_map/mul | solution.py:122
  352.4 71.4 %reshape.23 = f32[2,4,64,4,64,4]{5,4,3,2,1,0:T(8,128)} reshape(f32[8,256,256]{2,1,0:T(8,128)} %fusion.68) | data formatting | bytes 4194304 | tf_op jit(solution)/shard_map/reshape | solution.py:79
  423.8 20.8 %reduce_sum.36 = f32[2,64,64]{2,1,0:T(8,128)S(1)} reduce(f32[2,4,64,4,64,4]{5,4,3,2,1,0:T(8,128)} %reshape.23, f32[]{:T(128)} %constant.83.clone.1), dimensions={1,3,5}, to_apply=%region_5.6 | reduce | flops 516096 | bytes 2129924 | tf_op jit(solution)/shard_map/reduce_sum | solution.py:79
  444.7 38.5 %all-reduce.47 = (f32[2,4096]{1,0:T(2,128)S(1)}, f32[1]{0:T(128)}) all-reduce(f32[2,4096]{1,0:T(2,128)S(1)} %mul.858, f32[1]{0:T(128)} %bitcast.9), channel_id=1, replica_groups=mesh['scen'=8,'slab'=16] {'scen'}, use_global_device_ids=true, to_apply=%region_6.7 | all-reduce | flops 8193 | bytes 65544 | tf_op jit(solution)/shard_map/psum | solution.py:123
  (86 shorter events, 20.7 us)
Async XLA Ops:
  1.7 135.9 %collective-permute-start = (f32[1,256,256]{2,1,0:T(8,128)S(1)}, f32[1,256,256]{2,1,0:T(8,128)S(1)}, u32[]{:S(2)}, u32[]{:S(2)}) collective-permute-start(f32[1,256,256]{2,1,0:T(8,128)S(1)} %get-tuple-element.75), channel_id=1, source_target_pairs={{1,0},{2,1},{3,2},{4,3},{5,4},{6,5},{7,6},{8,7},{9,8},{10,9},{11,1... | collective-permute-start | bytes 786440 | tf_op jit(solution)/shard_map/ppermute | solution.py:25
  3.6 134.0 %collective-permute-start.1 = (f32[1,256,256]{2,1,0:T(8,128)S(1)}, f32[1,256,256]{2,1,0:T(8,128)S(1)}, u32[]{:S(2)}, u32[]{:S(2)}) collective-permute-start(f32[1,256,256]{2,1,0:T(8,128)S(1)} %get-tuple-element.76), channel_id=1, source_target_pairs={{0,1},{1,2},{2,3},{3,4},{4,5},{5,6},{6,7},{7,8},{8,9},{9,10},{10,1... | collective-permute-start | bytes 786440 | tf_op jit(solution)/shard_map/ppermute | solution.py:23
  6.8 52.4 %copy-start.22 = (f32[1,2,4096]{2,1,0:T(2,128)}, f32[1,2,4096]{2,1,0:T(2,128)S(1)}, u32[]{:S(2)}) copy-start(f32[1,2,4096]{2,1,0:T(2,128)S(1)} %add.433) | copy-start | bytes 98308
  47.9 11.3 %copy-start.24 = (f32[2,4096]{1,0:T(2,128)}, f32[2,4096]{1,0:T(2,128)S(1)}, u32[]{:S(2)}) copy-start(f32[2,4096]{1,0:T(2,128)S(1)} %psum.35) | copy-start | bytes 98308
  137.6 16.4 %copy-start = (f32[1,8,256,256]{3,2,1,0:T(8,128)S(1)}, f32[1,8,256,256]{3,2,1,0:T(8,128)}, u32[]{:S(2)}) copy-start(f32[1,8,256,256]{3,2,1,0:T(8,128)} %param.10) | copy-start | bytes 6291460
  137.7 16.4 %copy-start.1 = (f32[1,8,256,256]{3,2,1,0:T(8,128)S(1)}, f32[1,8,256,256]{3,2,1,0:T(8,128)}, u32[]{:S(2)}) copy-start(f32[1,8,256,256]{3,2,1,0:T(8,128)} %param.9) | copy-start | bytes 6291460
  149.7 9.7 %copy-start.11 = (f32[8,256,256]{2,1,0:T(8,128)}, f32[8,256,256]{2,1,0:T(8,128)S(1)}, u32[]{:S(2)}) copy-start(f32[8,256,256]{2,1,0:T(8,128)S(1)} %get-tuple-element.43) | copy-start | bytes 6291460
  149.7 36.4 %copy-start.4 = (f32[8,256,256]{2,1,0:T(8,128)}, f32[8,256,256]{2,1,0:T(8,128)S(1)}, u32[]{:S(2)}) copy-start(f32[8,256,256]{2,1,0:T(8,128)S(1)} %get-tuple-element.44) | copy-start | bytes 6291460
  149.7 8.5 %collective-permute-start.2 = (f32[1,256,256]{2,1,0:T(8,128)S(1)}, f32[1,256,256]{2,1,0:T(8,128)S(1)}, u32[]{:S(2)}, u32[]{:S(2)}) collective-permute-start(f32[1,256,256]{2,1,0:T(8,128)S(1)} %get-tuple-element.71), channel_id=1, source_target_pairs={{1,0},{2,1},{3,2},{4,3},{5,4},{6,5},{7,6},{8,7},{9,8},{10,9},{11,1... | collective-permute-start | bytes 786440 | tf_op jit(solution)/shard_map/ppermute | solution.py:25
  151.7 7.7 %collective-permute-start.3 = (f32[1,256,256]{2,1,0:T(8,128)S(1)}, f32[1,256,256]{2,1,0:T(8,128)S(1)}, u32[]{:S(2)}, u32[]{:S(2)}) collective-permute-start(f32[1,256,256]{2,1,0:T(8,128)S(1)} %get-tuple-element.72), channel_id=1, source_target_pairs={{0,1},{1,2},{2,3},{3,4},{4,5},{5,6},{6,7},{7,8},{8,9},{9,10},{10,1... | collective-permute-start | bytes 786440 | tf_op jit(solution)/shard_map/ppermute | solution.py:23
  162.5 9.8 %copy-start.7 = (f32[8,256,256]{2,1,0:T(8,128)}, f32[8,256,256]{2,1,0:T(8,128)S(1)}, u32[]{:S(2)}) copy-start(f32[8,256,256]{2,1,0:T(8,128)S(1)} %fusion.15) | copy-start | bytes 6291460
  162.6 9.6 %collective-permute-start.4 = (f32[1,256,256]{2,1,0:T(8,128)S(1)}, f32[1,256,256]{2,1,0:T(8,128)S(1)}, u32[]{:S(2)}, u32[]{:S(2)}) collective-permute-start(f32[1,256,256]{2,1,0:T(8,128)S(1)} %get-tuple-element.67), channel_id=1, source_target_pairs={{1,0},{2,1},{3,2},{4,3},{5,4},{6,5},{7,6},{8,7},{9,8},{10,9},{11,1... | collective-permute-start | bytes 786440 | tf_op jit(solution)/shard_map/ppermute | solution.py:25
  164.7 7.7 %collective-permute-start.5 = (f32[1,256,256]{2,1,0:T(8,128)S(1)}, f32[1,256,256]{2,1,0:T(8,128)S(1)}, u32[]{:S(2)}, u32[]{:S(2)}) collective-permute-start(f32[1,256,256]{2,1,0:T(8,128)S(1)} %get-tuple-element.68), channel_id=1, source_target_pairs={{0,1},{1,2},{2,3},{3,4},{4,5},{5,6},{6,7},{7,8},{8,9},{9,10},{10,1... | collective-permute-start | bytes 786440 | tf_op jit(solution)/shard_map/ppermute | solution.py:23
  175.4 10.7 %copy-start.9 = (f32[8,256,256]{2,1,0:T(8,128)}, f32[8,256,256]{2,1,0:T(8,128)S(1)}, u32[]{:S(2)}) copy-start(f32[8,256,256]{2,1,0:T(8,128)S(1)} %fusion.23) | copy-start | bytes 6291460
  175.5 10.6 %collective-permute-start.6 = (f32[1,256,256]{2,1,0:T(8,128)S(1)}, f32[1,256,256]{2,1,0:T(8,128)S(1)}, u32[]{:S(2)}, u32[]{:S(2)}) collective-permute-start(f32[1,256,256]{2,1,0:T(8,128)S(1)} %get-tuple-element.65), channel_id=1, source_target_pairs={{1,0},{2,1},{3,2},{4,3},{5,4},{6,5},{7,6},{8,7},{9,8},{10,9},{11,1... | collective-permute-start | bytes 786440 | tf_op jit(solution)/shard_map/ppermute | solution.py:25
  177.9 8.3 %collective-permute-start.7 = (f32[1,256,256]{2,1,0:T(8,128)S(1)}, f32[1,256,256]{2,1,0:T(8,128)S(1)}, u32[]{:S(2)}, u32[]{:S(2)}) collective-permute-start(f32[1,256,256]{2,1,0:T(8,128)S(1)} %get-tuple-element.66), channel_id=1, source_target_pairs={{0,1},{1,2},{2,3},{3,4},{4,5},{5,6},{6,7},{7,8},{8,9},{9,10},{10,1... | collective-permute-start | bytes 786440 | tf_op jit(solution)/shard_map/ppermute | solution.py:23
  232.9 16.4 %collective-permute-start.8 = (f32[1,256,256]{2,1,0:T(8,128)S(1)}, f32[1,256,256]{2,1,0:T(8,128)S(1)}, u32[]{:S(2)}, u32[]{:S(2)}) collective-permute-start(f32[1,256,256]{2,1,0:T(8,128)S(1)} %get-tuple-element.61), channel_id=1, source_target_pairs={{1,0},{2,1},{3,2},{4,3},{5,4},{6,5},{7,6},{8,7},{9,8},{10,9},{11,1... | collective-permute-start | bytes 786440 | tf_op jit(solution)/shard_map/ppermute | solution.py:25
  238.2 11.1 %collective-permute-start.9 = (f32[1,256,256]{2,1,0:T(8,128)S(1)}, f32[1,256,256]{2,1,0:T(8,128)S(1)}, u32[]{:S(2)}, u32[]{:S(2)}) collective-permute-start(f32[1,256,256]{2,1,0:T(8,128)S(1)} %get-tuple-element.62), channel_id=1, source_target_pairs={{0,1},{1,2},{2,3},{3,4},{4,5},{5,6},{6,7},{7,8},{8,9},{9,10},{10,1... | collective-permute-start | bytes 786440 | tf_op jit(solution)/shard_map/ppermute | solution.py:23
  249.3 16.8 %copy-start.3 = (f32[1,8,256,256]{3,2,1,0:T(8,128)S(1)}, f32[1,8,256,256]{3,2,1,0:T(8,128)}, u32[]{:S(2)}) copy-start(f32[1,8,256,256]{3,2,1,0:T(8,128)} %param.9) | copy-start | bytes 6291460
  249.3 16.8 %copy-start.8 = (f32[8,256,256]{2,1,0:T(8,128)S(1)}, f32[8,256,256]{2,1,0:T(8,128)}, u32[]{:S(2)}) copy-start(f32[8,256,256]{2,1,0:T(8,128)} %copy-done.7) | copy-start | bytes 6291460
  274.5 14.3 %copy-start.19 = (f32[8,256,256]{2,1,0:T(8,128)}, f32[8,256,256]{2,1,0:T(8,128)S(1)}, u32[]{:S(2)}) copy-start(f32[8,256,256]{2,1,0:T(8,128)S(1)} %get-tuple-element.25) | copy-start | bytes 6291460
  274.5 14.3 %copy-start.20 = (f32[8,256,256]{2,1,0:T(8,128)}, f32[8,256,256]{2,1,0:T(8,128)S(1)}, u32[]{:S(2)}) copy-start(f32[8,256,256]{2,1,0:T(8,128)S(1)} %get-tuple-element.48) | copy-start | bytes 6291460
  274.5 14.2 %collective-permute-start.10 = (f32[1,256,256]{2,1,0:T(8,128)S(1)}, f32[1,256,256]{2,1,0:T(8,128)S(1)}, u32[]{:S(2)}, u32[]{:S(2)}) collective-permute-start(f32[1,256,256]{2,1,0:T(8,128)S(1)} %get-tuple-element.57), channel_id=1, source_target_pairs={{1,0},{2,1},{3,2},{4,3},{5,4},{6,5},{7,6},{8,7},{9,8},{10,9},{11,1... | collective-permute-start | bytes 786440 | tf_op jit(solution)/shard_map/ppermute | solution.py:25
  278.2 10.6 %collective-permute-start.11 = (f32[1,256,256]{2,1,0:T(8,128)S(1)}, f32[1,256,256]{2,1,0:T(8,128)S(1)}, u32[]{:S(2)}, u32[]{:S(2)}) collective-permute-start(f32[1,256,256]{2,1,0:T(8,128)S(1)} %get-tuple-element.58), channel_id=1, source_target_pairs={{0,1},{1,2},{2,3},{3,4},{4,5},{5,6},{6,7},{7,8},{8,9},{9,10},{10,1... | collective-permute-start | bytes 786440 | tf_op jit(solution)/shard_map/ppermute | solution.py:23
  288.8 16.4 %copy-start.12 = (f32[8,256,256]{2,1,0:T(8,128)S(1)}, f32[8,256,256]{2,1,0:T(8,128)}, u32[]{:S(2)}) copy-start(f32[8,256,256]{2,1,0:T(8,128)} %copy-done.11) | copy-start | bytes 6291460
  315.4 15.8 %copy-start.15 = (f32[8,256,256]{2,1,0:T(8,128)}, f32[8,256,256]{2,1,0:T(8,128)S(1)}, u32[]{:S(2)}) copy-start(f32[8,256,256]{2,1,0:T(8,128)S(1)} %get-tuple-element.15) | copy-start | bytes 6291460
  315.4 15.8 %copy-start.16 = (f32[8,256,256]{2,1,0:T(8,128)}, f32[8,256,256]{2,1,0:T(8,128)S(1)}, u32[]{:S(2)}) copy-start(f32[8,256,256]{2,1,0:T(8,128)S(1)} %get-tuple-element.46) | copy-start | bytes 6291460
  316.8 14.3 %collective-permute-start.12 = (f32[1,256,256]{2,1,0:T(8,128)S(1)}, f32[1,256,256]{2,1,0:T(8,128)S(1)}, u32[]{:S(2)}, u32[]{:S(2)}) collective-permute-start(f32[1,256,256]{2,1,0:T(8,128)S(1)} %get-tuple-element.53), channel_id=1, source_target_pairs={{1,0},{2,1},{3,2},{4,3},{5,4},{6,5},{7,6},{8,7},{9,8},{10,9},{11,1... | collective-permute-start | bytes 786440 | tf_op jit(solution)/shard_map/ppermute | solution.py:25
  320.5 10.7 %collective-permute-start.13 = (f32[1,256,256]{2,1,0:T(8,128)S(1)}, f32[1,256,256]{2,1,0:T(8,128)S(1)}, u32[]{:S(2)}, u32[]{:S(2)}) collective-permute-start(f32[1,256,256]{2,1,0:T(8,128)S(1)} %get-tuple-element.54), channel_id=1, source_target_pairs={{0,1},{1,2},{2,3},{3,4},{4,5},{5,6},{6,7},{7,8},{8,9},{9,10},{10,1... | collective-permute-start | bytes 786440 | tf_op jit(solution)/shard_map/ppermute | solution.py:23
  322.6 8.5 %copy-start.6 = (f32[8,256,256]{2,1,0:T(8,128)S(1)}, f32[8,256,256]{2,1,0:T(8,128)}, u32[]{:S(2)}) copy-start(f32[8,256,256]{2,1,0:T(8,128)} %copy-done.4) | copy-start | bytes 6291460
  423.8 59.4 %copy-start.23 = (f32[1,2,4096]{2,1,0:T(2,128)S(1)}, f32[1,2,4096]{2,1,0:T(2,128)}, u32[]{:S(2)}) copy-start(f32[1,2,4096]{2,1,0:T(2,128)} %copy-done.22) | copy-start | bytes 98308
  423.8 59.4 %copy-start.25 = (f32[2,4096]{1,0:T(2,128)S(1)}, f32[2,4096]{1,0:T(2,128)}, u32[]{:S(2)}) copy-start(f32[2,4096]{1,0:T(2,128)} %copy-done.24) | copy-start | bytes 98308
  (8 other events, 57.9 us)
where the time goes:
time: 494 us; the launch traced here: 486 us
  other arithmetic  180 us (36%)
  local copies, waits for them, and re-layouts  152 us (31%)
  blocking collectives  107 us (22%)
  starting transfers between devices  39.9 us (8%)
  between operations  5.33 us (1%)
    reshape x1, local copies, waits for them, and re-layouts, restrict(): fine.reshape(plane_count // 4, 4, row_count // 4, 4, column_count // 4, 4)  71.4 us
    reshape x1, local copies, waits for them, and re-layouts, prolong(): return cube.reshape(plane_count * 4, row_count, column_count)  56.1 us
    psum x1, blocking collectives, on_device(): lax.psum(jnp.sum(control + multiplier, axis=0), 'scen') / scen_count  41.1 us
    psum x1, blocking collectives, on_device(): total = lax.psum(gradient, 'scen')  38.5 us
    mul x3, other arithmetic, horizontal(): return -advect + DIFF_FLAT * spread - rate * field  37.5 us
    psum x1, blocking collectives, on_device(): lax.psum((jnp.sum(monitor_float * field * field), jnp.sum(monitor_float))...  27.7 us
    add_any x3, other arithmetic, divergence(): product = backward * forward  26.7 us
    neg x3, other arithmetic, divergence(): backward = field - lower_cells  25.5 us
  transfers between devices with their start and end apart: 14, of which 2 were waited for; matrix products, arithmetic and copies ran while one was open for 26% of the time, Pallas kernels for 0%

commit v1 on v0

--- a/solution.py
+++ b/solution.py
@@ -120,7 +120,7 @@
         adjoint = adjoint + TIME_STEP * (pulled + DIFF_VERTICAL * vertical)
     coarse_cells = plane_count * slab_count * row_count * column_count / 64.0
     gradient = coarse_cells * restrict(wells_float * rate_grad)
-    total = lax.psum(gradient, "scen")
+    total = jnp.sum(lax.all_gather(gradient, "scen"), axis=0)
     consensus_next = consensus - total
     multiplier_next = multiplier + control - consensus_next[None]
     cvar = threshold + risk

time: 494 us -> 509 us (1.030)
  blocking collectives: 107 us -> 123 us
    all_gather x0 -> x1, blocking collectives: none -> 34.4 us  [on_device(): total = jnp.sum(lax.all_gather(gradient, 'scen'), axis=0)]
    psum x1, blocking collectives: 38.5 us -> 20.3 us  [on_device(): risk = lax.psum(soft_term, 'scen')]
  transfers between devices with their start and end apart: 14 -> 14, of which waited for: 2 -> 1; matrix products, arithmetic and copies ran while one was open for 26% -> 26% of each run, Pallas kernels for 0% -> 0%
where the time goes in v1:
time: 509 us; the launch traced here: 500 us
  other arithmetic  180 us (35%)
  local copies, waits for them, and re-layouts  152 us (30%)
  blocking collectives  123 us (24%)
  starting transfers between devices  37.9 us (7%)
  between operations  5.38 us (1%)
    reshape x1, local copies, waits for them, and re-layouts, restrict(): fine.reshape(plane_count // 4, 4, row_count // 4, 4, column_count // 4, 4)  71.4 us
    reshape x1, local copies, waits for them, and re-layouts, prolong(): return cube.reshape(plane_count * 4, row_count, column_count)  56.1 us
    psum x1, blocking collectives, on_device(): lax.psum(jnp.sum(control + multiplier, axis=0), 'scen') / scen_count  41.1 us
    mul x3, other arithmetic, horizontal(): return -advect + DIFF_FLAT * spread - rate * field  37.5 us
    all_gather x1, blocking collectives, on_device(): total = jnp.sum(lax.all_gather(gradient, 'scen'), axis=0)  34.4 us
    psum x1, blocking collectives, on_device(): lax.psum((jnp.sum(monitor_float * field * field), jnp.sum(monitor_float))...  27.5 us
    add_any x3, other arithmetic, divergence(): product = backward * forward  26.8 us
    neg x3, other arithmetic, divergence(): backward = field - lower_cells  25.6 us
  transfers between devices with their start and end apart: 14, of which 1 were waited for; matrix products, arithmetic and copies ran while one was open for 26% of the time, Pallas kernels for 0%

profile of v1, /device:TPU:2, one launch (start us, length us, event | category | flops | bytes accessed | tf_op | source)
XLA Modules:
  0.0 500.2 jit_solution(14629804327878242146)
XLA Ops:
  3.6 2.4 collective-permute-start.1
  6.9 41.1 %psum.28 = f32[2,4096]{1,0:T(2,128)S(1)} all-reduce(f32[2,4096]{1,0:T(2,128)S(1)} %bitcast.40), channel_id=1, replica_groups=mesh['scen'=8,'slab'=16] {'scen'}, use_global_device_ids=true, to_apply=%region_0.0 | all-reduce | flops 8192 | bytes 65536 | tf_op jit(solution)/shard_map/psum | solution.py:88
  48.0 11.3 %bitcast_multiply_fusion.3 = (f32[8,256,256]{2,1,0:T(8,128)}, f32[8,256,256]{2,1,0:T(8,128)}) fusion(f32[1,8,256,256]{3,2,1,0:T(8,128)} %param.10, f32[8,256,256]{2,1,0:T(8,128)} %bitcast.37, f32[1,8,256,256]{3,2,1,0:T(8,128)} %param.9), kind=kLoop, calls=%fused_computation.197 | loop fusion | flops 18874368 | bytes 10485760 | tf_op jit(solution)/shard_map/mul | solution.py:57
  59.4 21.5 %broadcast_in_dim.17 = f32[2,4,64,4,64,4]{5,4,3,2,1,0:T(8,128)} broadcast(f32[2,64,64]{2,1,0:T(8,128)S(1)} %broadcast_in_dim.16), dimensions={0,2,4} | broadcast | bytes 2129920 | tf_op jit(solution)/shard_map/broadcast_in_dim | solution.py:73
  81.0 56.1 %reshape.32 = f32[8,256,256]{2,1,0:T(8,128)} reshape(f32[2,4,64,4,64,4]{5,4,3,2,1,0:T(8,128)} %broadcast_in_dim.17) | data formatting | bytes 4194304 | tf_op jit(solution)/shard_map/reshape | solution.py:74
  137.7 12.0 %fusion.7 = (f32[8,256,256]{2,1,0:T(8,128)S(1)}, f32[8,256,256]{2,1,0:T(8,128)S(1)}) fusion(f32[8,256,256]{2,1,0:T(8,128)} %bitcast.38, f32[8,256,256]{2,1,0:T(8,128)} %get-tuple-element.76, f32[8,256,256]{2,1,0:T(8,128)} %get-tuple-element.75, f32[1,256,256]{2,1,0:T(8,128)S(1)} %collective-permute-done.1, f32[1,256,256]{2,1,0:T(8,128)S(1)} %collective-permute-done, ...), kind=kLoop, calls=%fused_computation.48 | loop fusion | flops 12582912 | bytes 15204352 | tf_op jit(solution)/shard_map/add | solution.py:101
  154.2 4.1 bitcast_multiply_fusion.2
  159.4 3.2 fusion.15
  164.7 3.5 collective-permute-start.5
  168.3 4.1 bitcast_multiply_fusion.1
  172.5 3.1 fusion.23
  175.6 2.5 collective-permute-start.6
  178.1 4.1 collective-permute-start.7
  182.2 4.1 bitcast_multiply_fusion.4
  186.4 5.1 %fusion.42 = (f32[]{:T(128)}, f32[]{:T(128)}, f32[8,256,256]{2,1,0:T(8,128)}) fusion(s32[8,256,256]{2,1,0:T(8,128)S(1)} %copy-done.21, f32[8,256,256]{2,1,0:T(8,128)S(1)} %fusion.23, f32[1,256,256]{2,1,0:T(8,128)S(1)} %collective-permute-done.7, f32[1,256,256]{2,1,0:T(8,128)S(1)} %collective-permute-done.6, f32[8,256,256]{2,1,0:T(8,128)S(1)} %get-tuple-element.42, ...), kind=kLoop, calls=%fused_computation.83 | loop fusion | flops 14155774 | bytes 13107208 | tf_op jit(solution)/shard_map/reduce_sum | solution.py:104
  191.5 27.5 %all-reduce.46 = (f32[]{:T(128)}, f32[]{:T(128)}) all-reduce(f32[]{:T(128)} %get-tuple-element.5, f32[]{:T(128)} %get-tuple-element.4), channel_id=1, replica_groups=mesh['scen'=8,'slab'=16] {'slab'}, use_global_device_ids=true, to_apply=%region_4.5 | all-reduce | flops 2 | bytes 16 | tf_op jit(solution)/shard_map/psum | solution.py:104
  220.3 4.3 broadcast_multiply_fusion.2
  224.7 8.3 %fusion.45 = (f32[8,256,256]{2,1,0:T(8,128)}, f32[8,256,256]{2,1,0:T(8,128)S(1)}, f32[8,256,256]{2,1,0:T(8,128)}, f32[8,256,256]{2,1,0:T(8,128)S(1)}) fusion(f32[8,256,256]{2,1,0:T(8,128)S(1)} %copy-done.10, f32[8,256,256]{2,1,0:T(8,128)S(1)} %get-tuple-element.31, f32[1,8,256,256]{3,2,1,0:T(8,128)S(1)} %copy-done, f32[1,8,256,256]{3,2,1,0:T(8,128)S(1)} %copy-done.2), kind=kLoop, calls=%fused_computation.86 | loop fusion | flops 39321600 | bytes 16777216 | tf_op jit(solution)/shard_map/transpose(jvp())/add_any | solution.py:52
  233.0 5.5 %collective-permute-start.8 = (f32[1,256,256]{2,1,0:T(8,128)S(1)}, f32[1,256,256]{2,1,0:T(8,128)S(1)}, u32[]{:S(2)}, u32[]{:S(2)}) collective-permute-start(f32[1,256,256]{2,1,0:T(8,128)S(1)} %get-tuple-element.59), channel_id=1, source_target_pairs={{1,0},{2,1},{3,2},{4,3},{5,4},{6,5},{7,6},{8,7},{9,8},{10,9},{11,1... | collective-permute-start | bytes 786440 | tf_op jit(solution)/shard_map/ppermute | solution.py:25
  240.4 8.6 %fusion.190 = (f32[8,256,256]{2,1,0:T(8,128)}, f32[8,256,256]{2,1,0:T(8,128)}, f32[8,256,256]{2,1,0:T(8,128)}, f32[8,256,256]{2,1,0:T(8,128)}) fusion(f32[8,256,256]{2,1,0:T(8,128)S(1)} %get-tuple-element.33, f32[8,256,256]{2,1,0:T(8,128)S(1)} %copy-done.10, f32[8,256,256]{2,1,0:T(8,128)S(1)} %get-tuple-element.48), kind=kLoop, calls=%fused_computation.312 | loop fusion | flops 37748736 | bytes 14680064 | tf_op jit(solution)/shard_map/transpose(jvp())/neg | solution.py:50
  249.1 20.3 %psum.31 = f32[1]{0:T(128)} all-reduce(f32[1]{0:T(128)} %bitcast.9), channel_id=1, replica_groups=mesh['scen'=8,'slab'=16] {'scen'}, use_global_device_ids=true, to_apply=%region_7.8 | all-reduce | flops 1 | bytes 8 | tf_op jit(solution)/shard_map/psum | solution.py:110
  270.1 16.5 %broadcast_multiply_fusion.1 = (f32[8,256,256]{2,1,0:T(8,128)}, f32[8,256,256]{2,1,0:T(8,128)S(1)}) fusion(f32[8,256,256]{2,1,0:T(8,128)} %copy-done.13, f32[1,256,256]{2,1,0:T(8,128)S(1)} %collective-permute-done.9, f32[1,256,256]{2,1,0:T(8,128)S(1)} %collective-permute-done.8, f32[8,256,256]{2,1,0:T(8,128)} %get-tuple-element.57, ...), kind=kLoop, calls=%fused_computation.294 | loop fusion | flops 16777216 | bytes 27787264 | tf_op jit(solution)/shard_map/transpose(jvp())/mul | solution.py:67
  286.6 8.3 %fusion.51 = (f32[8,256,256]{2,1,0:T(8,128)}, f32[8,256,256]{2,1,0:T(8,128)S(1)}, f32[8,256,256]{2,1,0:T(8,128)}, f32[8,256,256]{2,1,0:T(8,128)S(1)}) fusion(f32[8,256,256]{2,1,0:T(8,128)S(1)} %copy-done.8, f32[8,256,256]{2,1,0:T(8,128)S(1)} %get-tuple-element.21, f32[1,8,256,256]{3,2,1,0:T(8,128)S(1)} %copy-done, f32[1,8,256,256]{3,2,1,0:T(8,128)S(1)} %copy-done.3), kind=kLoop, calls=%fused_computation.92 | loop fusion | flops 39321600 | bytes 16777216 | tf_op jit(solution)/shard_map/transpose(jvp())/add_any | solution.py:52
  299.4 8.5 %fusion.184 = (f32[8,256,256]{2,1,0:T(8,128)}, f32[8,256,256]{2,1,0:T(8,128)}, f32[8,256,256]{2,1,0:T(8,128)}, f32[8,256,256]{2,1,0:T(8,128)}) fusion(f32[8,256,256]{2,1,0:T(8,128)S(1)} %get-tuple-element.23, f32[8,256,256]{2,1,0:T(8,128)S(1)} %copy-done.8, f32[8,256,256]{2,1,0:T(8,128)S(1)} %get-tuple-element.46), kind=kLoop, calls=%fused_computation.310 | loop fusion | flops 37748736 | bytes 14680064 | tf_op jit(solution)/shard_map/transpose(jvp())/neg | solution.py:50
  307.9 16.7 %broadcast_multiply_fusion = (f32[8,256,256]{2,1,0:T(8,128)}, f32[8,256,256]{2,1,0:T(8,128)}) fusion(f32[8,256,256]{2,1,0:T(8,128)} %copy-done.14, f32[1,256,256]{2,1,0:T(8,128)S(1)} %collective-permute-done.11, f32[1,256,256]{2,1,0:T(8,128)S(1)} %collective-permute-done.10, f32[8,256,256]{2,1,0:T(8,128)} %get-tuple-element.53, ...), kind=kLoop, calls=%fused_computation.293 | loop fusion | flops 16777216 | bytes 27787264 | tf_op jit(solution)/shard_map/transpose(jvp())/mul | solution.py:67
  324.5 10.3 %fusion.57 = (f32[8,256,256]{2,1,0:T(8,128)}, f32[8,256,256]{2,1,0:T(8,128)S(1)}, f32[8,256,256]{2,1,0:T(8,128)}, f32[8,256,256]{2,1,0:T(8,128)S(1)}) fusion(f32[8,256,256]{2,1,0:T(8,128)S(1)} %copy-done.12, f32[8,256,256]{2,1,0:T(8,128)} %get-tuple-element.11, f32[1,8,256,256]{3,2,1,0:T(8,128)S(1)} %copy-done, f32[1,8,256,256]{3,2,1,0:T(8,128)S(1)} %copy-done.3), kind=kLoop, calls=%fused_computation.98 | loop fusion | flops 39321600 | bytes 16777216 | tf_op jit(solution)/shard_map/transpose(jvp())/add_any | solution.py:52
  336.2 3.2 collective-permute-start.12
  341.6 8.5 %fusion.177 = (f32[8,256,256]{2,1,0:T(8,128)}, f32[8,256,256]{2,1,0:T(8,128)}, f32[8,256,256]{2,1,0:T(8,128)}, f32[8,256,256]{2,1,0:T(8,128)}) fusion(f32[8,256,256]{2,1,0:T(8,128)S(1)} %get-tuple-element.13, f32[8,256,256]{2,1,0:T(8,128)S(1)} %copy-done.12, f32[8,256,256]{2,1,0:T(8,128)S(1)} %get-tuple-element.44), kind=kLoop, calls=%fused_computation.308 | loop fusion | flops 37748736 | bytes 14680064 | tf_op jit(solution)/shard_map/transpose(jvp())/neg | solution.py:50
  350.1 21.2 %fusion.68 = f32[8,256,256]{2,1,0:T(8,128)} fusion(f32[8,256,256]{2,1,0:T(8,128)} %get-tuple-element.11, f32[1,256,256]{2,1,0:T(8,128)S(1)} %collective-permute-done.13, f32[1,256,256]{2,1,0:T(8,128)S(1)} %collective-permute-done.12, f32[8,256,256]{2,1,0:T(8,128)} %get-tuple-element.49, f32[8,256,256]{2,1,0:T(8,128)} %get-tuple-element.43, ...), kind=kLoop, calls=%fused_computation.110 | loop fusion | flops 23592960 | bytes 40370176 | tf_op jit(solution)/shard_map/mul | solution.py:122
  371.3 71.4 %reshape.33 = f32[2,4,64,4,64,4]{5,4,3,2,1,0:T(8,128)} reshape(f32[8,256,256]{2,1,0:T(8,128)} %fusion.68) | data formatting | bytes 4194304 | tf_op jit(solution)/shard_map/reshape | solution.py:79
  442.8 20.8 %reduce_sum.45 = f32[2,64,64]{2,1,0:T(8,128)S(1)} reduce(f32[2,4,64,4,64,4]{5,4,3,2,1,0:T(8,128)} %reshape.33, f32[]{:T(128)} %constant.83.clone.1), dimensions={1,3,5}, to_apply=%region_5.6 | reduce | flops 516096 | bytes 2129924 | tf_op jit(solution)/shard_map/reduce_sum | solution.py:79
  463.7 34.4 %all_gather.4 = f32[8,2,4096]{2,1,0:T(2,128)S(1)} all-gather(f32[1,2,4096]{2,1,0:T(2,128)S(1)} %mul.865), channel_id=1, replica_groups=mesh['scen'=8,'slab'=16] {'scen'}, dimensions={0}, use_global_device_ids=true | all-gather | bytes 294912 | tf_op jit(solution)/shard_map/all_gather | solution.py:123
  (88 shorter events, 22.4 us)
Async XLA Ops:
  1.7 136.0 %collective-permute-start = (f32[1,256,256]{2,1,0:T(8,128)S(1)}, f32[1,256,256]{2,1,0:T(8,128)S(1)}, u32[]{:S(2)}, u32[]{:S(2)}) collective-permute-start(f32[1,256,256]{2,1,0:T(8,128)S(1)} %get-tuple-element.73), channel_id=1, source_target_pairs={{1,0},{2,1},{3,2},{4,3},{5,4},{6,5},{7,6},{8,7},{9,8},{10,9},{11,1... | collective-permute-start | bytes 786440 | tf_op jit(solution)/shard_map/ppermute | solution.py:25
  3.6 134.1 %collective-permute-start.1 = (f32[1,256,256]{2,1,0:T(8,128)S(1)}, f32[1,256,256]{2,1,0:T(8,128)S(1)}, u32[]{:S(2)}, u32[]{:S(2)}) collective-permute-start(f32[1,256,256]{2,1,0:T(8,128)S(1)} %get-tuple-element.74), channel_id=1, source_target_pairs={{0,1},{1,2},{2,3},{3,4},{4,5},{5,6},{6,7},{7,8},{8,9},{9,10},{10,1... | collective-permute-start | bytes 786440 | tf_op jit(solution)/shard_map/ppermute | solution.py:23
  6.8 52.4 %copy-start.22 = (f32[1,2,4096]{2,1,0:T(2,128)}, f32[1,2,4096]{2,1,0:T(2,128)S(1)}, u32[]{:S(2)}) copy-start(f32[1,2,4096]{2,1,0:T(2,128)S(1)} %add.431) | copy-start | bytes 98308
  47.9 11.3 %copy-start.24 = (f32[2,4096]{1,0:T(2,128)}, f32[2,4096]{1,0:T(2,128)S(1)}, u32[]{:S(2)}) copy-start(f32[2,4096]{1,0:T(2,128)S(1)} %psum.28) | copy-start | bytes 98308
  137.7 16.5 %copy-start = (f32[1,8,256,256]{3,2,1,0:T(8,128)S(1)}, f32[1,8,256,256]{3,2,1,0:T(8,128)}, u32[]{:S(2)}) copy-start(f32[1,8,256,256]{3,2,1,0:T(8,128)} %param.10) | copy-start | bytes 6291460
  137.7 16.5 %copy-start.1 = (f32[1,8,256,256]{3,2,1,0:T(8,128)S(1)}, f32[1,8,256,256]{3,2,1,0:T(8,128)}, u32[]{:S(2)}) copy-start(f32[1,8,256,256]{3,2,1,0:T(8,128)} %param.9) | copy-start | bytes 6291460
  149.7 9.7 %copy-start.11 = (f32[8,256,256]{2,1,0:T(8,128)}, f32[8,256,256]{2,1,0:T(8,128)S(1)}, u32[]{:S(2)}) copy-start(f32[8,256,256]{2,1,0:T(8,128)S(1)} %get-tuple-element.41) | copy-start | bytes 6291460
  149.7 36.6 %copy-start.4 = (f32[8,256,256]{2,1,0:T(8,128)}, f32[8,256,256]{2,1,0:T(8,128)S(1)}, u32[]{:S(2)}) copy-start(f32[8,256,256]{2,1,0:T(8,128)S(1)} %get-tuple-element.42) | copy-start | bytes 6291460
  149.8 8.5 %collective-permute-start.2 = (f32[1,256,256]{2,1,0:T(8,128)S(1)}, f32[1,256,256]{2,1,0:T(8,128)S(1)}, u32[]{:S(2)}, u32[]{:S(2)}) collective-permute-start(f32[1,256,256]{2,1,0:T(8,128)S(1)} %get-tuple-element.69), channel_id=1, source_target_pairs={{1,0},{2,1},{3,2},{4,3},{5,4},{6,5},{7,6},{8,7},{9,8},{10,9},{11,1... | collective-permute-start | bytes 786440 | tf_op jit(solution)/shard_map/ppermute | solution.py:25
  151.7 7.7 %collective-permute-start.3 = (f32[1,256,256]{2,1,0:T(8,128)S(1)}, f32[1,256,256]{2,1,0:T(8,128)S(1)}, u32[]{:S(2)}, u32[]{:S(2)}) collective-permute-start(f32[1,256,256]{2,1,0:T(8,128)S(1)} %get-tuple-element.70), channel_id=1, source_target_pairs={{0,1},{1,2},{2,3},{3,4},{4,5},{5,6},{6,7},{7,8},{8,9},{9,10},{10,1... | collective-permute-start | bytes 786440 | tf_op jit(solution)/shard_map/ppermute | solution.py:23
  162.6 9.9 %copy-start.7 = (f32[8,256,256]{2,1,0:T(8,128)}, f32[8,256,256]{2,1,0:T(8,128)S(1)}, u32[]{:S(2)}) copy-start(f32[8,256,256]{2,1,0:T(8,128)S(1)} %fusion.15) | copy-start | bytes 6291460
  162.6 9.8 %collective-permute-start.4 = (f32[1,256,256]{2,1,0:T(8,128)S(1)}, f32[1,256,256]{2,1,0:T(8,128)S(1)}, u32[]{:S(2)}, u32[]{:S(2)}) collective-permute-start(f32[1,256,256]{2,1,0:T(8,128)S(1)} %get-tuple-element.65), channel_id=1, source_target_pairs={{1,0},{2,1},{3,2},{4,3},{5,4},{6,5},{7,6},{8,7},{9,8},{10,9},{11,1... | collective-permute-start | bytes 786440 | tf_op jit(solution)/shard_map/ppermute | solution.py:25
  164.7 7.7 %collective-permute-start.5 = (f32[1,256,256]{2,1,0:T(8,128)S(1)}, f32[1,256,256]{2,1,0:T(8,128)S(1)}, u32[]{:S(2)}, u32[]{:S(2)}) collective-permute-start(f32[1,256,256]{2,1,0:T(8,128)S(1)} %get-tuple-element.66), channel_id=1, source_target_pairs={{0,1},{1,2},{2,3},{3,4},{4,5},{5,6},{6,7},{7,8},{8,9},{9,10},{10,1... | collective-permute-start | bytes 786440 | tf_op jit(solution)/shard_map/ppermute | solution.py:23
  175.5 10.8 %copy-start.9 = (f32[8,256,256]{2,1,0:T(8,128)}, f32[8,256,256]{2,1,0:T(8,128)S(1)}, u32[]{:S(2)}) copy-start(f32[8,256,256]{2,1,0:T(8,128)S(1)} %fusion.23) | copy-start | bytes 6291460
  175.6 10.8 %collective-permute-start.6 = (f32[1,256,256]{2,1,0:T(8,128)S(1)}, f32[1,256,256]{2,1,0:T(8,128)S(1)}, u32[]{:S(2)}, u32[]{:S(2)}) collective-permute-start(f32[1,256,256]{2,1,0:T(8,128)S(1)} %get-tuple-element.63), channel_id=1, source_target_pairs={{1,0},{2,1},{3,2},{4,3},{5,4},{6,5},{7,6},{8,7},{9,8},{10,9},{11,1... | collective-permute-start | bytes 786440 | tf_op jit(solution)/shard_map/ppermute | solution.py:25
  178.1 8.3 %collective-permute-start.7 = (f32[1,256,256]{2,1,0:T(8,128)S(1)}, f32[1,256,256]{2,1,0:T(8,128)S(1)}, u32[]{:S(2)}, u32[]{:S(2)}) collective-permute-start(f32[1,256,256]{2,1,0:T(8,128)S(1)} %get-tuple-element.64), channel_id=1, source_target_pairs={{0,1},{1,2},{2,3},{3,4},{4,5},{5,6},{6,7},{7,8},{8,9},{9,10},{10,1... | collective-permute-start | bytes 786440 | tf_op jit(solution)/shard_map/ppermute | solution.py:23
  233.0 37.0 %collective-permute-start.8 = (f32[1,256,256]{2,1,0:T(8,128)S(1)}, f32[1,256,256]{2,1,0:T(8,128)S(1)}, u32[]{:S(2)}, u32[]{:S(2)}) collective-permute-start(f32[1,256,256]{2,1,0:T(8,128)S(1)} %get-tuple-element.59), channel_id=1, source_target_pairs={{1,0},{2,1},{3,2},{4,3},{5,4},{6,5},{7,6},{8,7},{9,8},{10,9},{11,1... | collective-permute-start | bytes 786440 | tf_op jit(solution)/shard_map/ppermute | solution.py:25
  238.5 31.5 %collective-permute-start.9 = (f32[1,256,256]{2,1,0:T(8,128)S(1)}, f32[1,256,256]{2,1,0:T(8,128)S(1)}, u32[]{:S(2)}, u32[]{:S(2)}) collective-permute-start(f32[1,256,256]{2,1,0:T(8,128)S(1)} %get-tuple-element.60), channel_id=1, source_target_pairs={{0,1},{1,2},{2,3},{3,4},{4,5},{5,6},{6,7},{7,8},{8,9},{9,10},{10,1... | collective-permute-start | bytes 786440 | tf_op jit(solution)/shard_map/ppermute | solution.py:23
  270.0 16.6 %copy-start.3 = (f32[1,8,256,256]{3,2,1,0:T(8,128)S(1)}, f32[1,8,256,256]{3,2,1,0:T(8,128)}, u32[]{:S(2)}) copy-start(f32[1,8,256,256]{3,2,1,0:T(8,128)} %param.9) | copy-start | bytes 6291460
  270.0 16.6 %copy-start.8 = (f32[8,256,256]{2,1,0:T(8,128)S(1)}, f32[8,256,256]{2,1,0:T(8,128)}, u32[]{:S(2)}) copy-start(f32[8,256,256]{2,1,0:T(8,128)} %copy-done.7) | copy-start | bytes 6291460
  294.9 12.9 %copy-start.19 = (f32[8,256,256]{2,1,0:T(8,128)}, f32[8,256,256]{2,1,0:T(8,128)S(1)}, u32[]{:S(2)}) copy-start(f32[8,256,256]{2,1,0:T(8,128)S(1)} %get-tuple-element.23) | copy-start | bytes 6291460
  294.9 12.9 %copy-start.20 = (f32[8,256,256]{2,1,0:T(8,128)}, f32[8,256,256]{2,1,0:T(8,128)S(1)}, u32[]{:S(2)}) copy-start(f32[8,256,256]{2,1,0:T(8,128)S(1)} %get-tuple-element.46) | copy-start | bytes 6291460
  295.0 12.8 %collective-permute-start.10 = (f32[1,256,256]{2,1,0:T(8,128)S(1)}, f32[1,256,256]{2,1,0:T(8,128)S(1)}, u32[]{:S(2)}, u32[]{:S(2)}) collective-permute-start(f32[1,256,256]{2,1,0:T(8,128)S(1)} %get-tuple-element.55), channel_id=1, source_target_pairs={{1,0},{2,1},{3,2},{4,3},{5,4},{6,5},{7,6},{8,7},{9,8},{10,9},{11,1... | collective-permute-start | bytes 786440 | tf_op jit(solution)/shard_map/ppermute | solution.py:25
  296.9 10.9 %collective-permute-start.11 = (f32[1,256,256]{2,1,0:T(8,128)S(1)}, f32[1,256,256]{2,1,0:T(8,128)S(1)}, u32[]{:S(2)}, u32[]{:S(2)}) collective-permute-start(f32[1,256,256]{2,1,0:T(8,128)S(1)} %get-tuple-element.56), channel_id=1, source_target_pairs={{0,1},{1,2},{2,3},{3,4},{4,5},{5,6},{6,7},{7,8},{8,9},{9,10},{10,1... | collective-permute-start | bytes 786440 | tf_op jit(solution)/shard_map/ppermute | solution.py:23
  307.9 16.7 %copy-start.12 = (f32[8,256,256]{2,1,0:T(8,128)S(1)}, f32[8,256,256]{2,1,0:T(8,128)}, u32[]{:S(2)}) copy-start(f32[8,256,256]{2,1,0:T(8,128)} %copy-done.11) | copy-start | bytes 6291460
  334.8 15.3 %copy-start.15 = (f32[8,256,256]{2,1,0:T(8,128)}, f32[8,256,256]{2,1,0:T(8,128)S(1)}, u32[]{:S(2)}) copy-start(f32[8,256,256]{2,1,0:T(8,128)S(1)} %get-tuple-element.13) | copy-start | bytes 6291460
  334.8 15.3 %copy-start.16 = (f32[8,256,256]{2,1,0:T(8,128)}, f32[8,256,256]{2,1,0:T(8,128)S(1)}, u32[]{:S(2)}) copy-start(f32[8,256,256]{2,1,0:T(8,128)S(1)} %get-tuple-element.44) | copy-start | bytes 6291460
  336.2 13.9 %collective-permute-start.12 = (f32[1,256,256]{2,1,0:T(8,128)S(1)}, f32[1,256,256]{2,1,0:T(8,128)S(1)}, u32[]{:S(2)}, u32[]{:S(2)}) collective-permute-start(f32[1,256,256]{2,1,0:T(8,128)S(1)} %get-tuple-element.51), channel_id=1, source_target_pairs={{1,0},{2,1},{3,2},{4,3},{5,4},{6,5},{7,6},{8,7},{9,8},{10,9},{11,1... | collective-permute-start | bytes 786440 | tf_op jit(solution)/shard_map/ppermute | solution.py:25
  339.4 10.7 %collective-permute-start.13 = (f32[1,256,256]{2,1,0:T(8,128)S(1)}, f32[1,256,256]{2,1,0:T(8,128)S(1)}, u32[]{:S(2)}, u32[]{:S(2)}) collective-permute-start(f32[1,256,256]{2,1,0:T(8,128)S(1)} %get-tuple-element.52), channel_id=1, source_target_pairs={{0,1},{1,2},{2,3},{3,4},{4,5},{5,6},{6,7},{7,8},{8,9},{9,10},{10,1... | collective-permute-start | bytes 786440 | tf_op jit(solution)/shard_map/ppermute | solution.py:23
  341.5 8.6 %copy-start.6 = (f32[8,256,256]{2,1,0:T(8,128)S(1)}, f32[8,256,256]{2,1,0:T(8,128)}, u32[]{:S(2)}) copy-start(f32[8,256,256]{2,1,0:T(8,128)} %copy-done.4) | copy-start | bytes 6291460
  442.8 55.4 %copy-start.23 = (f32[1,2,4096]{2,1,0:T(2,128)S(1)}, f32[1,2,4096]{2,1,0:T(2,128)}, u32[]{:S(2)}) copy-start(f32[1,2,4096]{2,1,0:T(2,128)} %copy-done.22) | copy-start | bytes 98308
  442.8 55.4 %copy-start.25 = (f32[2,4096]{1,0:T(2,128)S(1)}, f32[2,4096]{1,0:T(2,128)}, u32[]{:S(2)}) copy-start(f32[2,4096]{1,0:T(2,128)} %copy-done.24) | copy-start | bytes 98308
  (8 other events, 57.1 us)
